TPU v7x, 128 devices: a whole 4x4x4 slice. The times are simulated.
128 devices in a mesh: section: 4 (over z), dp: 8 (over y, core), mp: 4 (over x).
Axes of the slice: x: 4, y: 4, z: 4, core: 2. Of those that a mesh axis runs over, the one named last changes fastest.
Arguments:
- text: bfloat16 [4, 4096, 4096], P('section', ('dp', 'mp')), may hold values from -6 to 6
- patches: bfloat16 [16384, 1024], P(('section', 'dp')), may hold values from -6 to 6
- segments: int32 [4, 8, 512], P('section', 'dp'), may hold values from 0 to 3, never falling along the last dimension, each value on 1 to 256 neighbouring positions
- loss_mask: int32 [4, 4096], P('section', ('dp', 'mp')), may hold values from 0 to 1, as said below
- tile_batch: int32 [8, 8], P('dp'), may hold values from 0 to 3, as said below
- tile_offset: int32 [8, 8], P('dp'), may hold values from 0 to 448, as said below
- attn_gain: float32 [4, 4096], P('section'), may hold values from 0.5 to 2
- w_query: bfloat16 [4, 4096, 2048], P('section', None, 'mp'), may hold values from -0.09375 to 0.09375
- w_kv: bfloat16 [4, 2, 4096, 512], P('section', None, None, 'mp'), may hold values from -0.09375 to 0.09375
- w_out: bfloat16 [4, 2048, 4096], P('section', 'mp'), may hold values from -0.125 to 0.125
- vis_gain: float32 [2, 1024], replicated, may hold values from 0.5 to 2
- vis_bias: float32 [2, 1024], replicated, may hold values from -3 to 3
- v_qkv: bfloat16 [3, 1024, 1024], P(None, ('section', 'dp'), 'mp'), may hold values from -0.1875 to 0.1875
- v_out: bfloat16 [1024, 1024], P('mp', ('section', 'dp')), may hold values from -0.1875 to 0.1875
- v_up: bfloat16 [1024, 4096], P(('section', 'dp'), 'mp'), may hold values from -0.1875 to 0.1875
- v_down: bfloat16 [4096, 1024], P('mp', ('section', 'dp')), may hold values from -0.09375 to 0.09375
- v_proj: bfloat16 [4096, 4096], P(('section', 'dp'), 'mp'), may hold values from -0.09375 to 0.09375
Outputs:
- hidden: bfloat16 [4, 4096, 4096], P('section', ('dp', 'mp'))
- token_weight: float32 [4, 4096], P('section', ('dp', 'mp'))
Inputs may be any that keep to these rules, and one draw needn't show every extreme that they name: `tile_batch`: in every data-parallel index, the 2 tiles of each section index go 1 to each of two different micro-batches; one micro-batch receives 1 tiles from every section index. `tile_offset`: offsets are multiples of 64; the runs of one sequence never intersect. `loss_mask`: the first position of every sequence is a one.
All inputs are finite; a program needn't handle non-finite values.
Results may differ from a plain program's by a relative error of at most 0.025.
Values may be sent and summed in bfloat16 or wider, within the bound.
A program may use at most 192 MiB of HBM per device.

v0:
```python
import jax
import jax.numpy as jnp
from jax import lax
from jax.sharding import Mesh
from jax.sharding import PartitionSpec as P

HD = 128
VHD = 64
GRID = 16
PATCH = 256
POOL = 64
SECTION_DP = ("section", "dp_0", "dp_1")
SECTION_DP_MP = ("section", "dp_0", "dp_1", "mp")
DP = ("dp_0", "dp_1")
DP_MP = ("dp_0", "dp_1", "mp")
EPS = 1e-05
ROPE_BASE = 500000.0
BLOCKED = -1e30


def layer_norm(values, gain, bias):
    wide = values.astype(jnp.float32)
    center = wide - jnp.mean(wide, axis=-1, keepdims=True)
    spread = jnp.mean(center * center, axis=-1, keepdims=True)
    return (center * lax.rsqrt(spread + EPS) * gain + bias).astype(jnp.bfloat16)


def rms_norm(values, gain):
    wide = values.astype(jnp.float32)
    power = jnp.mean(wide * wide, axis=-1, keepdims=True)
    return (wide * lax.rsqrt(power + EPS) * gain).astype(jnp.bfloat16)


def pixel_shuffle(states):
    tile_count = states.shape[0] // PATCH
    side_half = GRID // 2
    width = states.shape[1]
    arranged = states.reshape(tile_count, side_half, 2, side_half, 2, width)
    return arranged.transpose(0, 1, 3, 2, 4, 5).reshape(
        tile_count * side_half * side_half, 4 * width
    )


def gathered(array, axis):
    copies = jnp.broadcast_to(array, (lax.axis_size(axis), *array.shape))
    return lax.all_to_all(copies, axis, split_axis=0, concat_axis=0, tiled=True)


def block_sum(partial_value):
    everything = gathered(partial_value.astype(jnp.bfloat16), "mp")
    return jnp.sum(everything.astype(jnp.float32), axis=0)


def transposed_dot(left, right):
    return lax.dot_general(
        left, right, (((1,), (1,)), ((), ())), preferred_element_type=jnp.float32
    )


def rope_tables(length):
    half_width = HD // 2
    freqs = ROPE_BASE ** (-2.0 * jnp.arange(half_width, dtype=jnp.float32) / HD)
    angles = jnp.arange(length, dtype=jnp.float32)[:, None] * freqs[None, :]
    cosine, sinus = (jnp.cos(angles), jnp.sin(angles))
    return (jnp.concatenate([cosine, cosine], axis=1), jnp.concatenate([-sinus, sinus], axis=1))


def encode_tiles(patches, vis_gain, vis_bias, small, proj_full):
    tile_count = patches.shape[0] // PATCH
    width = patches.shape[1]
    local = width // lax.axis_size("mp")
    head_count = local // VHD
    normed = layer_norm(patches, vis_gain[0], vis_bias[0])
    joined = jnp.dot(normed, small[:, : 3 * local], preferred_element_type=jnp.float32)
    joined = joined.astype(jnp.bfloat16).reshape(tile_count, PATCH, 3, head_count, VHD)
    query, keyed, valued = (joined[:, :, index] for index in range(3))
    scores = jnp.einsum("tqhd,tkhd->thqk", query, keyed, preferred_element_type=jnp.float32)
    probs = jax.nn.softmax(scores * VHD ** (-0.5), axis=-1).astype(jnp.bfloat16)
    mixed = jnp.einsum("thqk,tkhd->tqhd", probs, valued, preferred_element_type=jnp.float32)
    mixed = mixed.astype(jnp.bfloat16).reshape(tile_count * PATCH, local)
    attended = block_sum(transposed_dot(mixed, small[:, 3 * local : 4 * local]))
    residual = (patches.astype(jnp.float32) + attended).astype(jnp.bfloat16)
    normed_two = layer_norm(residual, vis_gain[1], vis_bias[1])
    hidden = small.shape[1] // 2 - 2 * local
    up = small[:, 4 * local : 4 * local + hidden]
    down = small[:, 4 * local + hidden :]
    inner = jax.nn.gelu(
        jnp.dot(normed_two, up, preferred_element_type=jnp.float32), approximate=False
    ).astype(jnp.bfloat16)
    fed = block_sum(transposed_dot(inner, down))
    states = (residual.astype(jnp.float32) + fed).astype(jnp.bfloat16)
    return jnp.dot(pixel_shuffle(states), proj_full, preferred_element_type=jnp.float32).astype(
        jnp.bfloat16
    )


def decoder_layer(state, allowed, cosine, sinus, w_joined, w_out):
    blocks = gathered(state, "mp")
    count, length, block_width = blocks.shape
    query_width = w_out.shape[0] // count
    rows = jnp.moveaxis(blocks, 0, 1).reshape(length, count * block_width)
    wide = rows.astype(jnp.float32)
    scale = lax.rsqrt(jnp.mean(wide * wide, axis=-1, keepdims=True) + EPS)
    joined = jnp.dot(rows, w_joined, preferred_element_type=jnp.float32) * scale
    heads = joined.reshape(length, joined.shape[1] // HD, HD)
    turned = heads * cosine[:, None] + jnp.roll(heads, HD // 2, axis=-1) * sinus[:, None]
    query_heads = query_width // HD
    query = turned[:, :query_heads].astype(jnp.bfloat16)
    keyed = turned[:, query_heads].astype(jnp.bfloat16)
    valued = heads[:, query_heads + 1].astype(jnp.bfloat16)
    scores = jnp.einsum("qgd,sd->gqs", query, keyed, preferred_element_type=jnp.float32)
    scores = jnp.where(allowed, scores * HD ** (-0.5), BLOCKED)
    probs = jax.nn.softmax(scores, axis=-1).astype(jnp.bfloat16)
    mixed = (
        jnp.einsum("gqs,sd->qgd", probs, valued, preferred_element_type=jnp.float32)
        .astype(jnp.bfloat16)
        .reshape(length, query_width)
    )
    parts = jnp.moveaxis(gathered(mixed, "mp"), 0, 1).reshape(length, count * query_width)
    added = jnp.dot(parts, w_out, preferred_element_type=jnp.float32)
    return (state.astype(jnp.float32) + added).astype(jnp.bfloat16)


def shards(
    text,
    patches,
    segments,
    loss_mask,
    tile_batch,
    tile_offset,
    attn_gain,
    w_query,
    w_kv,
    w_out,
    vis_gain,
    vis_bias,
    v_qkv,
    v_out,
    v_up,
    v_down,
    v_proj,
):
    sections = lax.axis_size("section")
    section_at = lax.axis_index("section")
    parts = lax.axis_size("mp")
    copies = lax.axis_size(DP)
    copy_at = lax.axis_index(DP)
    small = jnp.concatenate([v_qkv[0], v_qkv[1], v_qkv[2], v_out.T, v_up, v_down.T], axis=1)
    small = lax.all_gather(small, SECTION_DP, axis=0, tiled=True)
    proj_full = lax.all_gather(v_proj, SECTION_DP, axis=0, tiled=True)
    model_width = w_query.shape[1]
    row_share = model_width // copies
    pick = lambda array: lax.dynamic_slice_in_dim(array, copy_at * row_share, row_share, 0)
    own_rows = jnp.concatenate([pick(w_query[0]), pick(w_kv[0, 0]), pick(w_kv[0, 1])], axis=1)
    own_gain = lax.dynamic_slice_in_dim(attn_gain[0], copy_at * row_share, row_share, 0)
    own_rows = (own_rows.astype(jnp.float32) * own_gain[:, None]).astype(jnp.bfloat16)
    block_width = model_width // parts
    col_share = block_width // copies
    own_out = w_out[0].reshape(w_out.shape[1], parts, copies, col_share)
    own_out = lax.dynamic_slice_in_dim(own_out, copy_at, 1, 2)[:, :, 0]
    own_out = lax.all_to_all(
        jnp.moveaxis(own_out, 1, 0), "mp", split_axis=0, concat_axis=0, tiled=True
    )
    joined_all = lax.all_gather(own_rows, SECTION_DP).reshape(
        sections, model_width, own_rows.shape[1]
    )
    out_all = lax.all_gather(own_out, SECTION_DP).reshape(
        sections, copies, parts * w_out.shape[1], col_share
    )
    text_blocks = lax.all_to_all(
        jnp.moveaxis(text[0].reshape(text.shape[1], parts, block_width), 1, 0),
        "mp",
        split_axis=0,
        concat_axis=0,
        tiled=True,
    ).reshape(text.shape[1] * parts, block_width)
    embedded = encode_tiles(patches, vis_gain, vis_bias, small, proj_full)
    length = segments.shape[2]
    tiles_here = embedded.shape[0] // POOL
    batch_all = tile_batch[0]
    offset_all = tile_offset[0]
    own_batch = lax.dynamic_slice_in_dim(batch_all, section_at * tiles_here, tiles_here, 0)
    capacity = tiles_here // 2
    block_rows = capacity * POOL
    local_ids = jnp.arange(tiles_here, dtype=jnp.int32)
    local_same = (own_batch[:, None] == own_batch[None, :]) & (
        local_ids[None, :] < local_ids[:, None]
    )
    local_rank = jnp.sum(local_same.astype(jnp.int32), axis=1)
    send_rows = jnp.arange(sections * block_rows, dtype=jnp.int32)
    send_target = send_rows // block_rows
    send_rank = send_rows % block_rows // POOL
    send_match = (own_batch[None, :] == send_target[:, None]) & (
        local_rank[None, :] == send_rank[:, None]
    )
    own_rows = jnp.arange(tiles_here * POOL, dtype=jnp.int32)
    send_pick = jnp.repeat(send_match, POOL, axis=1) & (
        (own_rows % POOL)[None, :] == (send_rows % POOL)[:, None]
    )
    blocks = jnp.dot(
        send_pick.astype(jnp.bfloat16), embedded, preferred_element_type=jnp.float32
    ).astype(jnp.bfloat16)
    arrived = lax.all_to_all(blocks, "section", split_axis=0, concat_axis=0, tiled=True)
    tile_ids = jnp.arange(batch_all.shape[0], dtype=jnp.int32)
    source_ids = tile_ids // tiles_here
    tile_same = (
        (batch_all[:, None] == batch_all[None, :])
        & (source_ids[:, None] == source_ids[None, :])
        & (tile_ids[None, :] < tile_ids[:, None])
    )
    tile_rank = jnp.sum(tile_same.astype(jnp.int32), axis=1)
    slot_rows = jnp.arange(sections * block_rows, dtype=jnp.int32)
    slot_source = slot_rows // block_rows
    slot_rank = slot_rows % block_rows // POOL
    match = (
        (batch_all[None, :] == section_at)
        & (source_ids[None, :] == slot_source[:, None])
        & (tile_rank[None, :] == slot_rank[:, None])
    )
    slot_place = jnp.sum(match.astype(jnp.int32) * offset_all[None, :], axis=1) + slot_rows % POOL
    slot_valid = jnp.any(match, axis=1)
    places = jnp.arange(length, dtype=jnp.int32)
    picker = ((places[:, None] == slot_place[None, :]) & slot_valid[None, :]).astype(jnp.bfloat16)
    image_cols = jnp.dot(picker, arrived, preferred_element_type=jnp.float32).astype(jnp.bfloat16)
    covered = jnp.any(
        (batch_all[None, :] == section_at)
        & (places[:, None] >= offset_all[None, :])
        & (places[:, None] < offset_all[None, :] + POOL),
        axis=1,
    )
    state = jnp.where(covered[:, None], image_cols, text_blocks)
    segment_ids = segments[0, 0]
    allowed = (segment_ids[:, None] == segment_ids[None, :]) & (places[None, :] <= places[:, None])
    cosine, sinus = rope_tables(length)
    for layer in range(sections):
        w_layer = jnp.moveaxis(out_all[layer], 0, 1).reshape(out_all.shape[2], block_width)
        state = decoder_layer(state, allowed, cosine, sinus, joined_all[layer], w_layer)
    hidden = lax.all_to_all(
        state.reshape(parts, length // parts, block_width),
        "mp",
        split_axis=0,
        concat_axis=0,
        tiled=True,
    )
    hidden = jnp.moveaxis(hidden, 0, 1).reshape(length // parts, model_width)
    totals = lax.psum(jnp.sum(loss_mask), SECTION_DP_MP)
    scaling = float(sections * lax.axis_size(DP) * length)
    token_weight = loss_mask.astype(jnp.float32) * scaling / totals.astype(jnp.float32)
    return (hidden[None], token_weight)


def solution(mesh):
    split = Mesh(
        mesh.devices.reshape(mesh.shape["section"], 4, 2, mesh.shape["mp"]),
        ("section", "dp_0", "dp_1", "mp"),
    )
    return jax.shard_map(
        shards,
        mesh=split,
        in_specs=(
            P("section", DP_MP, None),
            P(SECTION_DP, None),
            P("section", DP, None),
            P("section", DP_MP),
            P(DP, None),
            P(DP, None),
            P("section", None),
            P("section", None, "mp"),
            P("section", None, None, "mp"),
            P("section", "mp", None),
            P(),
            P(),
            P(None, SECTION_DP, "mp"),
            P("mp", SECTION_DP),
            P(SECTION_DP, "mp"),
            P("mp", SECTION_DP),
            P(SECTION_DP, "mp"),
        ),
        out_specs=(P("section", DP_MP, None), P("section", DP_MP)),
        check_vma=False,
    )
```

profile of v0, /device:TPU:1, one launch (start us, length us, event | category | flops | bytes accessed | tf_op | source)
XLA Modules:
  0.0 700.2 jit_solution(4039534892102669239)
XLA Ops:
  17.3 6.5 copy.169
  25.3 13.5 %all_to_all.77 = bf16[4,512,128]{2,1,0:T(8,128)(2,1)} all-to-all(bf16[4,512,128]{2,1,0:T(8,128)(2,1)S(1)} %bitcast.271), channel_id=1, replica_groups=mesh['section'=4,'dp_0'=4,'dp_1'=2,'mp'=4] {'mp'}, dimensions={0} | all-to-all | bytes 1048576 | tf_op jit(solution)/shard_map/all_to_all | solution.py:161
  39.5 25.9 %all-gather.6.cloned.1.call-done = bf16[1024,3072]{1,0:T(8,128)(2,1)} async-done(((bf16[32,3072]{1,0:T(8,128)(2,1)}), bf16[1024,3072]{1,0:T(8,128)(2,1)}) %all-gather.6.cloned.1.call-update) | async-done | bytes 6291472 | tf_op jit(solution)/shard_map/all_gather | solution.py:149
  65.4 2.5 fusion.67
  79.7 52.3 %all_to_all.78 = bf16[4,512,1024]{2,1,0:T(8,128)(2,1)S(1)} all-to-all(bf16[4,512,1024]{2,1,0:T(8,128)(2,1)S(1)} %broadcast_in_dim.44), channel_id=1, replica_groups=mesh['section'=4,'dp_0'=4,'dp_1'=2,'mp'=4] {'mp'}, dimensions={0} | all-to-all | bytes 8388608 | tf_op jit(solution)/shard_map/all_to_all | solution.py:46
  133.7 8.5 %fusion.64 = bf16[512,1024]{1,0:T(8,128)(2,1)S(1)} fusion(bf16[1024,3072]{1,0:T(8,128)(2,1)} %all-gather.6.cloned.1.call-done, bf16[512,1024]{1,0:T(8,128)(2,1)S(1)} %get-tuple-element.3, f32[1024]{0:T(1024)S(1)} %bitcast.283, f32[1024]{0:T(1024)S(1)} %bitcast.282, f32[512]{0:T(512)S(1)} %add_rsqrt_fusion.4, f32[512]{0:T(512)S(1)} %broadcast_multiply_fusion), kind=kOutput, calls=%fused_computation.109 | convolution fusion | flops 2185232384 | bytes 6303744 | tf_op jit(solution)/shard_map/dot_general | solution.py:55
  142.2 2.5 broadcast_in_dim.45
  144.7 5.0 all-to-all-start.1
  152.6 44.7 %all-to-all-done.1 = bf16[4,512,1024]{2,1,0:T(8,128)(2,1)} async-done(((bf16[4,512,1024]{2,1,0:T(8,128)(2,1)}), bf16[4,512,1024]{2,1,0:T(8,128)(2,1)}, u32[]{:S(2)}, u32[]{:S(2)}) %all-to-all-start.1) | async-done | bytes 4194336 | tf_op jit(solution)/shard_map/all_to_all | solution.py:46
  197.3 4.5 all-to-all-start.3
  201.8 3.7 convert_reduce_fusion
  208.0 5.7 convolution_convert_fusion.2
  214.7 3.5 all-to-all-start.2
  218.4 6.7 all-to-all-done.2
  227.4 2.2 broadcast_in_dim.46
  229.7 5.3 all-to-all-start.4
  236.5 43.3 %all-to-all-done.4 = bf16[4,512,1024]{1,2,0:T(8,128)(2,1)} async-done(((bf16[4,512,1024]{1,2,0:T(8,128)(2,1)}), bf16[4,512,1024]{1,2,0:T(8,128)(2,1)}, u32[]{:S(2)}, u32[]{:S(2)}) %all-to-all-start.4) | async-done | bytes 4194336 | tf_op jit(solution)/shard_map/all_to_all | solution.py:46
  279.7 3.1 multiply_reduce_fusion.3
  282.9 16.0 %fusion.218 = (bf16[8,512,768]{2,1,0:T(8,128)(2,1)}, bf16[8,512,768]{2,1,0:T(8,128)(2,1)}, bf16[8,512,768]{2,1,0:T(8,128)(2,1)}, bf16[8,512,768]{2,1,0:T(8,128)(2,1)S(1)}) fusion(bf16[32,512,768]{2,1,0:T(8,128)(2,1)} %all-gather.10.cloned.1.call-done), kind=kLoop, calls=%fused_computation.300 | loop fusion | bytes 50331648 | tf_op jit(solution)/shard_map/slice | solution.py:237
  298.9 5.3 convolution_multiply_fusion.3
  314.5 4.4 all-to-all-start.5
  319.0 12.2 %fusion.219 = (bf16[32,512,128]{2,1,0:T(8,128)(2,1)}, bf16[32,512,128]{2,1,0:T(8,128)(2,1)}, bf16[32,512,128]{2,1,0:T(8,128)(2,1)}, bf16[32,512,128]{2,1,0:T(8,128)(2,1)}) fusion(bf16[128,512,128]{2,1,0:T(8,128)(2,1)} %all-gather.12.cloned.1.call-done), kind=kLoop, calls=%fused_computation.301 | loop fusion | bytes 33554432 | tf_op jit(solution)/shard_map/slice | solution.py:236
  331.2 6.5 copy.171
  337.7 2.7 all-to-all-done.5
  340.4 6.2 add_convert_fusion.3
  348.4 45.9 %all_to_all.79 = bf16[4,512,1024]{1,2,0:T(8,128)(2,1)S(1)} all-to-all(bf16[4,512,1024]{1,2,0:T(8,128)(2,1)S(1)} %broadcast_in_dim.52), channel_id=1, replica_groups=mesh['section'=4,'dp_0'=4,'dp_1'=2,'mp'=4] {'mp'}, dimensions={0} | all-to-all | bytes 8388608 | tf_op jit(solution)/shard_map/all_to_all | solution.py:46
  395.3 3.5 convolution_multiply_fusion.2
  404.1 2.1 fusion.234
  409.2 4.4 all-to-all-start.8
  413.6 6.6 copy.178
  420.2 12.8 %all-to-all-done.8 = bf16[4,512,512]{1,2,0:T(8,128)(2,1)} async-done(((bf16[4,512,512]{1,2,0:T(8,128)(2,1)}), bf16[4,512,512]{1,2,0:T(8,128)(2,1)}, u32[]{:S(2)}, u32[]{:S(2)}) %all-to-all-start.8) | async-done | bytes 2097184 | tf_op jit(solution)/shard_map/all_to_all | solution.py:46
  433.0 5.2 add_convert_fusion.2
  439.2 43.9 %all_to_all.80 = bf16[4,512,1024]{1,2,0:T(8,128)(2,1)S(1)} all-to-all(bf16[4,512,1024]{1,2,0:T(8,128)(2,1)S(1)} %broadcast_in_dim.54), channel_id=1, replica_groups=mesh['section'=4,'dp_0'=4,'dp_1'=2,'mp'=4] {'mp'}, dimensions={0} | all-to-all | bytes 8388608 | tf_op jit(solution)/shard_map/all_to_all | solution.py:46
  484.1 3.5 convolution_multiply_fusion.1
  493.0 2.1 fusion.235
  498.0 4.5 all-to-all-start.10
  502.5 6.6 copy.185
  509.1 10.8 %all-to-all-done.10 = bf16[4,512,512]{1,2,0:T(8,128)(2,1)} async-done(((bf16[4,512,512]{1,2,0:T(8,128)(2,1)}), bf16[4,512,512]{1,2,0:T(8,128)(2,1)}, u32[]{:S(2)}, u32[]{:S(2)}) %all-to-all-start.10) | async-done | bytes 2097184 | tf_op jit(solution)/shard_map/all_to_all | solution.py:46
  519.9 5.2 add_convert_fusion.1
  526.0 41.8 %all_to_all.81 = bf16[4,512,1024]{1,2,0:T(8,128)(2,1)S(1)} all-to-all(bf16[4,512,1024]{1,2,0:T(8,128)(2,1)S(1)} %broadcast_in_dim.56), channel_id=1, replica_groups=mesh['section'=4,'dp_0'=4,'dp_1'=2,'mp'=4] {'mp'}, dimensions={0} | all-to-all | bytes 8388608 | tf_op jit(solution)/shard_map/all_to_all | solution.py:46
  568.7 3.5 convolution_multiply_fusion
  577.5 2.1 fusion.236
  582.7 3.6 all-to-all-start.12
  586.3 6.5 copy.192
  592.8 8.8 %all-to-all-done.12 = bf16[4,512,512]{1,2,0:T(8,128)(2,1)S(1)} async-done(((bf16[4,512,512]{1,2,0:T(8,128)(2,1)}), bf16[4,512,512]{1,2,0:T(8,128)(2,1)S(1)}, u32[]{:S(2)}, u32[]{:S(2)}) %all-to-all-start.12) | async-done | bytes 2097184 | tf_op jit(solution)/shard_map/all_to_all | solution.py:46
  601.6 5.5 add_convert_fusion
  607.1 3.6 all-to-all-start.13
  611.4 78.2 %psum.7 = s32[]{:T(128)} all-reduce(s32[]{:T(128)} %reduce_sum.189), channel_id=1, replica_groups=mesh['section'=4,'dp_0'=4,'dp_1'=2,'mp'=4] {'section','dp_0','dp_1','mp'}, use_global_device_ids=true, to_apply=%region_26.27 | all-reduce | flops 1 | bytes 8 | tf_op jit(solution)/shard_map/psum | solution.py:246
  (164 shorter events, 80.8 us)
Async XLA Ops:
  7.2 6.1 copy-start
  7.2 58.2 %all-gather.6.cloned.1.call-start = ((), (), s32[]{:S(2)}) async-start(), calls=%async_computation.14 | async-start | bytes 6488064 | tf_op jit(solution)/shard_map/all_gather | solution.py:149
  11.8 0.7 copy-start.7
  12.5 195.5 %all-gather.8.cloned.1.call-start = ((), (), s32[]{:S(2)}) async-start(), calls=%async_computation.15 | async-start | bytes 8650752 | tf_op jit(solution)/shard_map/all_gather | solution.py:150
  13.2 269.6 %all-gather.10.cloned.1.call-start = ((), (), s32[]{:S(2)}) async-start(), calls=%async_computation.16 | async-start | bytes 25952256 | tf_op jit(solution)/shard_map/all_gather | solution.py:164
  17.3 301.7 %all-gather.12.cloned.1.call-start = ((), (), s32[]{:S(2)}) async-start(), calls=%async_computation.17 | async-start | bytes 17301504 | tf_op jit(solution)/shard_map/all_gather | solution.py:167
  23.8 15.0 %copy-start.2 = (bf16[512,1024]{1,0:T(8,128)(2,1)S(1)}, bf16[512,1024]{1,0:T(8,128)(2,1)}, u32[]{:S(2)}) copy-start(bf16[512,1024]{1,0:T(8,128)(2,1)} %param.18) | copy-start | bytes 3145732
  25.2 14.2 %copy-start.9 = (f32[2,1024]{1,0:T(2,128)S(1)}, f32[2,1024]{1,0:T(2,128)}, u32[]{:S(2)}) copy-start(f32[2,1024]{1,0:T(2,128)} %param.27) | copy-start | bytes 24580
  25.3 14.2 %copy-start.10 = (f32[2,1024]{1,0:T(2,128)S(1)}, f32[2,1024]{1,0:T(2,128)}, u32[]{:S(2)}) copy-start(f32[2,1024]{1,0:T(2,128)} %param.28) | copy-start | bytes 24580
  144.7 5.0 copy-start.3
  144.7 52.5 %all-to-all-start.1 = ((bf16[4,512,1024]{2,1,0:T(8,128)(2,1)}), bf16[4,512,1024]{2,1,0:T(8,128)(2,1)}, u32[]{:S(2)}, u32[]{:S(2)}) async-start(bf16[4,512,1024]{2,1,0:T(8,128)(2,1)} %broadcast_in_dim.45), calls=%async_computation.1 | async-start | bytes 8388608 | tf_op jit(solution)/shard_map/all_to_all | solution.py:46
  149.7 2.1 copy-start.11
  149.7 2.8 copy-start.12
  197.3 17.5 %all-to-all-start.3 = ((bf16[4,128,1024]{2,1,0:T(8,128)(2,1)}), bf16[4,128,1024]{2,1,0:T(8,128)(2,1)}, u32[]{:S(2)}, u32[]{:S(2)}) async-start(bf16[4,128,1024]{2,1,0:T(8,128)(2,1)} %bitcast.236), calls=%async_computation.3 | async-start | bytes 2097152 | tf_op jit(solution)/shard_map/all_to_all | solution.py:170
  214.7 10.4 %all-to-all-start.2 = ((bf16[4,64,1024]{2,1,0:T(8,128)(2,1)}), bf16[4,64,1024]{2,1,0:T(8,128)(2,1)S(1)}, u32[]{:S(2)}, u32[]{:S(2)}) async-start(bf16[4,64,1024]{2,1,0:T(8,128)(2,1)} %bitcast.20), calls=%async_computation.2 | async-start | bytes 1048576 | tf_op jit(solution)/shard_map/all_to_all | solution.py:203
  229.7 50.0 %all-to-all-start.4 = ((bf16[4,512,1024]{1,2,0:T(8,128)(2,1)}), bf16[4,512,1024]{1,2,0:T(8,128)(2,1)}, u32[]{:S(2)}, u32[]{:S(2)}) async-start(bf16[4,512,1024]{1,2,0:T(8,128)(2,1)} %broadcast_in_dim.46), calls=%async_computation.4 | async-start | bytes 8388608 | tf_op jit(solution)/shard_map/all_to_all | solution.py:46
  235.0 1.2 copy-start.8
  314.5 25.8 %all-to-all-start.5 = ((bf16[4,512,512]{1,2,0:T(8,128)(2,1)}), bf16[4,512,512]{1,2,0:T(8,128)(2,1)}, u32[]{:S(2)}, u32[]{:S(2)}) async-start(bf16[4,512,512]{1,2,0:T(8,128)(2,1)} %broadcast_in_dim.49), calls=%async_computation.5 | async-start | bytes 4194304 | tf_op jit(solution)/shard_map/all_to_all | solution.py:46
  348.1 47.2 %slice-start.4 = ((s8[6291456]{0:T(1024)(128)(4,1)}), s8[4194304]{0:T(1024)(128)(4,1)S(1)}, s32[]{:S(2)}) async-start(s8[6291456]{0:T(1024)(128)(4,1)} %bitcast.251), calls=%async_computation.22 | async-start | bytes 8388608
  348.4 46.9 %slice-start.5 = ((s8[6291456]{0:T(1024)(128)(4,1)}), s8[2097152]{0:T(1024)(128)(4,1)S(1)}, s32[]{:S(2)}) async-start(s8[6291456]{0:T(1024)(128)(4,1)} %bitcast.251), calls=%async_computation.23 | async-start | bytes 4194304
  409.2 23.8 %all-to-all-start.8 = ((bf16[4,512,512]{1,2,0:T(8,128)(2,1)}), bf16[4,512,512]{1,2,0:T(8,128)(2,1)}, u32[]{:S(2)}, u32[]{:S(2)}) async-start(bf16[4,512,512]{1,2,0:T(8,128)(2,1)} %broadcast_in_dim.53), calls=%async_computation.8 | async-start | bytes 4194304 | tf_op jit(solution)/shard_map/all_to_all | solution.py:46
  413.6 19.4 %copy-start.4 = (bf16[512,1024]{1,0:T(8,128)(2,1)S(1)}, bf16[512,1024]{1,0:T(8,128)(2,1)}, u32[]{:S(2)}) copy-start(bf16[512,1024]{1,0:T(8,128)(2,1)} %add_convert_fusion.3) | copy-start | bytes 3145732
  438.2 1.0 copy-start.5
  438.8 45.3 %slice-start.2 = ((s8[6291456]{0:T(1024)(128)(4,1)}), s8[4194304]{0:T(1024)(128)(4,1)S(1)}, s32[]{:S(2)}) async-start(s8[6291456]{0:T(1024)(128)(4,1)} %bitcast.248), calls=%async_computation.20 | async-start | bytes 8388608
  439.2 44.9 %slice-start.3 = ((s8[6291456]{0:T(1024)(128)(4,1)}), s8[2097152]{0:T(1024)(128)(4,1)S(1)}, s32[]{:S(2)}) async-start(s8[6291456]{0:T(1024)(128)(4,1)} %bitcast.248), calls=%async_computation.21 | async-start | bytes 4194304
  498.0 21.8 %all-to-all-start.10 = ((bf16[4,512,512]{1,2,0:T(8,128)(2,1)}), bf16[4,512,512]{1,2,0:T(8,128)(2,1)}, u32[]{:S(2)}, u32[]{:S(2)}) async-start(bf16[4,512,512]{1,2,0:T(8,128)(2,1)} %broadcast_in_dim.55), calls=%async_computation.10 | async-start | bytes 4194304 | tf_op jit(solution)/shard_map/all_to_all | solution.py:46
  502.5 17.4 %copy-start.6 = (bf16[512,1024]{1,0:T(8,128)(2,1)S(1)}, bf16[512,1024]{1,0:T(8,128)(2,1)}, u32[]{:S(2)}) copy-start(bf16[512,1024]{1,0:T(8,128)(2,1)} %copy-done.5) | copy-start | bytes 3145732
  525.6 43.1 %slice-start = ((s8[6291456]{0:T(1024)(128)(4,1)}), s8[4194304]{0:T(1024)(128)(4,1)S(1)}, s32[]{:S(2)}) async-start(s8[6291456]{0:T(1024)(128)(4,1)} %bitcast.245), calls=%async_computation.18 | async-start | bytes 8388608
  526.0 42.8 %slice-start.1 = ((s8[6291456]{0:T(1024)(128)(4,1)}), s8[2097152]{0:T(1024)(128)(4,1)S(1)}, s32[]{:S(2)}) async-start(s8[6291456]{0:T(1024)(128)(4,1)} %bitcast.245), calls=%async_computation.19 | async-start | bytes 4194304
  582.7 18.9 %all-to-all-start.12 = ((bf16[4,512,512]{1,2,0:T(8,128)(2,1)}), bf16[4,512,512]{1,2,0:T(8,128)(2,1)S(1)}, u32[]{:S(2)}, u32[]{:S(2)}) async-start(bf16[4,512,512]{1,2,0:T(8,128)(2,1)} %broadcast_in_dim.57), calls=%async_computation.12 | async-start | bytes 4194304 | tf_op jit(solution)/shard_map/all_to_all | solution.py:46
  607.1 3.7 copy-start.13
  607.1 83.7 %all-to-all-start.13 = ((bf16[4,128,1024]{2,1,0:T(8,128)(2,1)}), bf16[4,128,1024]{2,1,0:T(8,128)(2,1)S(1)}, u32[]{:S(2)}, u32[]{:S(2)}) async-start(bf16[4,128,1024]{2,1,0:T(8,128)(2,1)} %bitcast.273), calls=%async_computation.13 | async-start | bytes 2097152 | tf_op jit(solution)/shard_map/all_to_all | solution.py:238
  690.8 2.4 copy-start.1
Sparse Core Ops, SparseCore 0:
  12.6 52.7 all-gather.5
  67.7 51.5 all-gather.7
  121.5 91.5 all-gather.9
  215.2 71.9 all-gather.11
where the time goes:
time: 708 us; the launch traced here: 700 us
  blocking collectives  276 us (39%)
  waiting for transfers between devices  157 us (22%)
  local copies, waits for them, and re-layouts  114 us (16%)
  matrix products  70.6 us (10%)
  starting transfers between devices  39.1 us (6%)
  other arithmetic  27.5 us (4%)
  between operations  15.7 us (2%)
    all_to_all x4, blocking collectives, gathered(): return lax.all_to_all(copies, axis, split_axis=0, concat_axis=0, tiled=True)  184 us
    all_to_all x6, waiting for transfers between devices, gathered(): return lax.all_to_all(copies, axis, split_axis=0, concat_axis=0, tiled=True)  123 us
    psum x1, blocking collectives, shards(): totals = lax.psum(jnp.sum(loss_mask), SECTION_DP_MP)  78.2 us
    all_to_all x6, starting transfers between devices, gathered(): return lax.all_to_all(copies, axis, split_axis=0, concat_axis=0, tiled=True)  27.3 us
    transpose x4, local copies, waits for them, and re-layouts, shards(): jnp.moveaxis(out_all[layer], 0, 1).reshape(out_all.shape[2], block_width)  26.2 us
    all_gather x1, waiting for transfers between devices, shards(): small = lax.all_gather(small, SECTION_DP, axis=0, tiled=True)  25.9 us
    dot_general x4, matrix products, decoder_layer(): added = jnp.dot(parts, w_out, preferred_element_type=jnp.float32)  22.1 us
    slice x1, local copies, waits for them, and re-layouts, shards(): joined_all[layer]  16 us
  transfers between devices with their start and end apart: 13, of which 9 were waited for; matrix products, arithmetic and copies ran while one was open for 19% of the time, Pallas kernels for 0%

commit v1 on v0

--- a/solution.py
+++ b/solution.py
@@ -146,7 +146,12 @@
     copies = lax.axis_size(DP)
     copy_at = lax.axis_index(DP)
     small = jnp.concatenate([v_qkv[0], v_qkv[1], v_qkv[2], v_out.T, v_up, v_down.T], axis=1)
-    small = lax.all_gather(small, SECTION_DP, axis=0, tiled=True)
+    small = jnp.concatenate(
+        lax.all_to_all(
+            jnp.stack([small for _ in range(lax.axis_size(SECTION_DP))]), SECTION_DP, 0, 0
+        ),
+        0,
+    )
     proj_full = lax.all_gather(v_proj, SECTION_DP, axis=0, tiled=True)
     model_width = w_query.shape[1]
     row_share = model_width // copies

time: 708 us -> 808 us (1.14)
  waiting for transfers between devices: 157 us -> 212 us
  blocking collectives: 276 us -> 305 us
  starting transfers between devices: 39.1 us -> 56.2 us
    all_to_all x0 -> x1, waiting for transfers between devices: none -> 86.5 us  [shards(): lax.all_to_all(jnp.stack([small for _ in range(lax.axis_size(SECTION_DP))...]
    psum x1, blocking collectives: 78.2 us -> 117 us  [shards(): totals = lax.psum(jnp.sum(loss_mask), SECTION_DP_MP)]
    all_gather x1 -> x0, waiting for transfers between devices: 25.9 us -> none  [shards(): small = lax.all_gather(small, SECTION_DP, axis=0, tiled=True)]
    all_to_all x6, waiting for transfers between devices: 123 us -> 111 us  [gathered(): return lax.all_to_all(copies, axis, split_axis=0, concat_axis=0, tiled=True)]
    all_to_all x0 -> x1, starting transfers between devices: none -> 10.1 us  [shards(): lax.all_to_all(jnp.stack([small for _ in range(lax.axis_size(SECTION_DP))...]
    all_to_all x4, blocking collectives: 184 us -> 175 us  [gathered(): return lax.all_to_all(copies, axis, split_axis=0, concat_axis=0, tiled=True)]
  transfers between devices with their start and end apart: 13 -> 13, of which waited for: 9 -> 8; matrix products, arithmetic and copies ran while one was open for 19% -> 17% of each run, Pallas kernels for 0% -> 0%
where the time goes in v1:
time: 808 us; the launch traced here: 800 us
  blocking collectives  305 us (38%)
  waiting for transfers between devices  212 us (26%)
  local copies, waits for them, and re-layouts  112 us (14%)
  matrix products  70.6 us (9%)
  starting transfers between devices  56.2 us (7%)
  other arithmetic  27.3 us (3%)
  between operations  15.8 us (2%)
    all_to_all x4, blocking collectives, gathered(): return lax.all_to_all(copies, axis, split_axis=0, concat_axis=0, tiled=True)  175 us
    psum x1, blocking collectives, shards(): totals = lax.psum(jnp.sum(loss_mask), SECTION_DP_MP)  117 us
    all_to_all x6, waiting for transfers between devices, gathered(): return lax.all_to_all(copies, axis, split_axis=0, concat_axis=0, tiled=True)  111 us
    all_to_all x1, waiting for transfers between devices, shards(): lax.all_to_all(jnp.stack([small for _ in range(lax.axis_size(SECTION_DP))...  86.5 us
    all_to_all x6, starting transfers between devices, gathered(): return lax.all_to_all(copies, axis, split_axis=0, concat_axis=0, tiled=True)  27.5 us
    transpose x4, local copies, waits for them, and re-layouts, shards(): jnp.moveaxis(out_all[layer], 0, 1).reshape(out_all.shape[2], block_width)  26.2 us
    dot_general x4, matrix products, decoder_layer(): added = jnp.dot(parts, w_out, preferred_element_type=jnp.float32)  22.1 us
  transfers between devices with their start and end apart: 13, of which 8 were waited for; matrix products, arithmetic and copies ran while one was open for 17% of the time, Pallas kernels for 0%

profile of v1, /device:TPU:1, one launch (start us, length us, event | category | flops | bytes accessed | tf_op | source)
XLA Modules:
  0.0 799.7 jit_solution(15561746464296306015)
XLA Ops:
  12.0 6.5 copy.169
  19.9 13.4 %all_to_all.82 = bf16[4,512,128]{2,1,0:T(8,128)(2,1)} all-to-all(bf16[4,512,128]{2,1,0:T(8,128)(2,1)S(1)} %bitcast.272), channel_id=1, replica_groups=mesh['section'=4,'dp_0'=4,'dp_1'=2,'mp'=4] {'mp'}, dimensions={0} | all-to-all | bytes 1048576 | tf_op jit(solution)/shard_map/all_to_all | solution.py:166
  33.4 3.4 stack.2
  36.8 10.1 %all-to-all-start = ((bf16[32,32,3072]{2,1,0:T(8,128)(2,1)}), bf16[32,32,3072]{2,1,0:T(8,128)(2,1)}, u32[]{:S(2)}, u32[]{:S(2)}) async-start(bf16[32,32,3072]{2,1,0:T(8,128)(2,1)} %stack.2), calls=%async_computation | async-start | bytes 12582912 | tf_op jit(solution)/shard_map/all_to_all | solution.py:150
  47.6 86.5 %all-to-all-done = bf16[32,32,3072]{2,1,0:T(8,128)(2,1)} async-done(((bf16[32,32,3072]{2,1,0:T(8,128)(2,1)}), bf16[32,32,3072]{2,1,0:T(8,128)(2,1)}, u32[]{:S(2)}, u32[]{:S(2)}) %all-to-all-start) | async-done | bytes 6291488 | tf_op jit(solution)/shard_map/all_to_all | solution.py:150
  134.1 2.5 fusion.67
  141.8 2.1 fusion.228
  148.5 47.1 %all_to_all.83 = bf16[4,512,1024]{2,1,0:T(8,128)(2,1)S(1)} all-to-all(bf16[4,512,1024]{2,1,0:T(8,128)(2,1)S(1)} %broadcast_in_dim.44), channel_id=1, replica_groups=mesh['section'=4,'dp_0'=4,'dp_1'=2,'mp'=4] {'mp'}, dimensions={0} | all-to-all | bytes 8388608 | tf_op jit(solution)/shard_map/all_to_all | solution.py:46
  197.4 8.6 %fusion.64 = bf16[512,1024]{1,0:T(8,128)(2,1)S(1)} fusion(bf16[1024,3072]{1,0:T(8,128)(2,1)} %bitcast.13, bf16[512,1024]{1,0:T(8,128)(2,1)S(1)} %get-tuple-element.3, f32[1024]{0:T(1024)S(1)} %bitcast.284, f32[1024]{0:T(1024)S(1)} %bitcast.283, f32[512]{0:T(512)S(1)} %add_rsqrt_fusion.4, f32[512]{0:T(512)S(1)} %broadcast_multiply_fusion), kind=kOutput, calls=%fused_computation.109 | convolution fusion | flops 2185232384 | bytes 6303744 | tf_op jit(solution)/shard_map/dot_general | solution.py:55
  205.9 2.5 broadcast_in_dim.45
  208.4 5.0 all-to-all-start.2
  216.3 38.8 %all-to-all-done.2 = bf16[4,512,1024]{2,1,0:T(8,128)(2,1)} async-done(((bf16[4,512,1024]{2,1,0:T(8,128)(2,1)}), bf16[4,512,1024]{2,1,0:T(8,128)(2,1)}, u32[]{:S(2)}, u32[]{:S(2)}) %all-to-all-start.2) | async-done | bytes 4194336 | tf_op jit(solution)/shard_map/all_to_all | solution.py:46
  255.1 4.5 all-to-all-start.4
  259.6 3.4 convert_reduce_fusion
  265.7 5.6 convolution_convert_fusion.2
  271.3 10.4 %all-to-all-start.3 = ((bf16[4,64,1024]{2,1,0:T(8,128)(2,1)}), bf16[4,64,1024]{2,1,0:T(8,128)(2,1)S(1)}, u32[]{:S(2)}, u32[]{:S(2)}) async-start(bf16[4,64,1024]{2,1,0:T(8,128)(2,1)} %bitcast.21), calls=%async_computation.3 | async-start | bytes 1048576 | tf_op jit(solution)/shard_map/all_to_all | solution.py:208
  281.9 13.7 %all-to-all-done.3 = bf16[4,64,1024]{2,1,0:T(8,128)(2,1)S(1)} async-done(((bf16[4,64,1024]{2,1,0:T(8,128)(2,1)}), bf16[4,64,1024]{2,1,0:T(8,128)(2,1)S(1)}, u32[]{:S(2)}, u32[]{:S(2)}) %all-to-all-start.3) | async-done | bytes 524320 | tf_op jit(solution)/shard_map/all_to_all | solution.py:208
  297.8 2.2 broadcast_in_dim.46
  300.1 5.5 all-to-all-start.5
  307.0 42.0 %all-to-all-done.5 = bf16[4,512,1024]{1,2,0:T(8,128)(2,1)} async-done(((bf16[4,512,1024]{1,2,0:T(8,128)(2,1)}), bf16[4,512,1024]{1,2,0:T(8,128)(2,1)}, u32[]{:S(2)}, u32[]{:S(2)}) %all-to-all-start.5) | async-done | bytes 4194336 | tf_op jit(solution)/shard_map/all_to_all | solution.py:46
  349.0 3.1 multiply_reduce_fusion.3
  352.1 15.8 %fusion.218 = (bf16[8,512,768]{2,1,0:T(8,128)(2,1)}, bf16[8,512,768]{2,1,0:T(8,128)(2,1)}, bf16[8,512,768]{2,1,0:T(8,128)(2,1)}, bf16[8,512,768]{2,1,0:T(8,128)(2,1)S(1)}) fusion(bf16[32,512,768]{2,1,0:T(8,128)(2,1)} %all-gather.7.cloned.1.call-done), kind=kLoop, calls=%fused_computation.300 | loop fusion | bytes 50331648 | tf_op jit(solution)/shard_map/slice | solution.py:242
  368.0 5.3 convolution_multiply_fusion.3
  378.5 2.1 fusion.233
  383.6 4.4 all-to-all-start.6
  388.1 12.2 %fusion.219 = (bf16[32,512,128]{2,1,0:T(8,128)(2,1)}, bf16[32,512,128]{2,1,0:T(8,128)(2,1)}, bf16[32,512,128]{2,1,0:T(8,128)(2,1)}, bf16[32,512,128]{2,1,0:T(8,128)(2,1)}) fusion(bf16[128,512,128]{2,1,0:T(8,128)(2,1)} %all-gather.9.cloned.1.call-done), kind=kLoop, calls=%fused_computation.301 | loop fusion | bytes 33554432 | tf_op jit(solution)/shard_map/slice | solution.py:241
  400.3 6.5 copy.171
  407.9 6.2 add_convert_fusion.3
  415.9 44.9 %all_to_all.84 = bf16[4,512,1024]{1,2,0:T(8,128)(2,1)S(1)} all-to-all(bf16[4,512,1024]{1,2,0:T(8,128)(2,1)S(1)} %broadcast_in_dim.52), channel_id=1, replica_groups=mesh['section'=4,'dp_0'=4,'dp_1'=2,'mp'=4] {'mp'}, dimensions={0} | all-to-all | bytes 8388608 | tf_op jit(solution)/shard_map/all_to_all | solution.py:46
  461.8 3.5 convolution_multiply_fusion.2
  475.6 4.4 all-to-all-start.9
  480.1 6.6 copy.178
  486.7 11.4 %all-to-all-done.9 = bf16[4,512,512]{1,2,0:T(8,128)(2,1)} async-done(((bf16[4,512,512]{1,2,0:T(8,128)(2,1)}), bf16[4,512,512]{1,2,0:T(8,128)(2,1)}, u32[]{:S(2)}, u32[]{:S(2)}) %all-to-all-start.9) | async-done | bytes 2097184 | tf_op jit(solution)/shard_map/all_to_all | solution.py:46
  498.1 5.2 add_convert_fusion.2
  504.3 42.5 %all_to_all.85 = bf16[4,512,1024]{1,2,0:T(8,128)(2,1)S(1)} all-to-all(bf16[4,512,1024]{1,2,0:T(8,128)(2,1)S(1)} %broadcast_in_dim.54), channel_id=1, replica_groups=mesh['section'=4,'dp_0'=4,'dp_1'=2,'mp'=4] {'mp'}, dimensions={0} | all-to-all | bytes 8388608 | tf_op jit(solution)/shard_map/all_to_all | solution.py:46
  547.7 3.5 convolution_multiply_fusion.1
  561.7 4.5 all-to-all-start.11
  566.1 6.6 copy.185
  572.7 9.4 %all-to-all-done.11 = bf16[4,512,512]{1,2,0:T(8,128)(2,1)} async-done(((bf16[4,512,512]{1,2,0:T(8,128)(2,1)}), bf16[4,512,512]{1,2,0:T(8,128)(2,1)}, u32[]{:S(2)}, u32[]{:S(2)}) %all-to-all-start.11) | async-done | bytes 2097184 | tf_op jit(solution)/shard_map/all_to_all | solution.py:46
  582.1 5.2 add_convert_fusion.1
  588.2 40.4 %all_to_all.86 = bf16[4,512,1024]{1,2,0:T(8,128)(2,1)S(1)} all-to-all(bf16[4,512,1024]{1,2,0:T(8,128)(2,1)S(1)} %broadcast_in_dim.56), channel_id=1, replica_groups=mesh['section'=4,'dp_0'=4,'dp_1'=2,'mp'=4] {'mp'}, dimensions={0} | all-to-all | bytes 8388608 | tf_op jit(solution)/shard_map/all_to_all | solution.py:46
  629.6 3.5 convolution_multiply_fusion
  643.5 3.6 all-to-all-start.13
  647.1 6.5 copy.192
  653.6 8.8 %all-to-all-done.13 = bf16[4,512,512]{1,2,0:T(8,128)(2,1)S(1)} async-done(((bf16[4,512,512]{1,2,0:T(8,128)(2,1)}), bf16[4,512,512]{1,2,0:T(8,128)(2,1)S(1)}, u32[]{:S(2)}, u32[]{:S(2)}) %all-to-all-start.13) | async-done | bytes 2097184 | tf_op jit(solution)/shard_map/all_to_all | solution.py:46
  662.4 5.5 add_convert_fusion
  668.0 3.6 all-to-all-start.14
  672.3 116.9 %psum.7 = s32[]{:T(128)} all-reduce(s32[]{:T(128)} %reduce_sum.189), channel_id=1, replica_groups=mesh['section'=4,'dp_0'=4,'dp_1'=2,'mp'=4] {'section','dp_0','dp_1','mp'}, use_global_device_ids=true, to_apply=%region_26.27 | all-reduce | flops 1 | bytes 8 | tf_op jit(solution)/shard_map/psum | solution.py:251
  (170 shorter events, 77.8 us)
Async XLA Ops:
  7.2 0.8 copy-start
  7.2 258.5 %all-gather.5.cloned.1.call-start = ((), (), s32[]{:S(2)}) async-start(), calls=%async_computation.15 | async-start | bytes 8650752 | tf_op jit(solution)/shard_map/all_gather | solution.py:155
  7.9 344.2 %all-gather.7.cloned.1.call-start = ((), (), s32[]{:S(2)}) async-start(), calls=%async_computation.16 | async-start | bytes 25952256 | tf_op jit(solution)/shard_map/all_gather | solution.py:169
  11.9 376.2 %all-gather.9.cloned.1.call-start = ((), (), s32[]{:S(2)}) async-start(), calls=%async_computation.17 | async-start | bytes 17301504 | tf_op jit(solution)/shard_map/all_gather | solution.py:172
  18.5 14.8 %copy-start.9 = (bf16[3,32,256]{2,1,0:T(8,128)(2,1)S(1)}, bf16[3,32,256]{2,1,0:T(8,128)(2,1)}, u32[]{:S(2)}) copy-start(bf16[3,32,256]{2,1,0:T(8,128)(2,1)} %param.29) | copy-start | bytes 147460
  18.5 14.8 %copy-start.10 = (bf16[256,32]{0,1:T(8,128)(2,1)S(1)}, bf16[256,32]{0,1:T(8,128)(2,1)}, u32[]{:S(2)}) copy-start(bf16[256,32]{0,1:T(8,128)(2,1)} %param.30) | copy-start | bytes 49156
  18.5 14.9 %copy-start.7 = (bf16[32,1024]{1,0:T(8,128)(2,1)S(1)}, bf16[32,1024]{1,0:T(8,128)(2,1)}, u32[]{:S(2)}) copy-start(bf16[32,1024]{1,0:T(8,128)(2,1)} %param.31) | copy-start | bytes 196612
  18.5 14.9 %copy-start.8 = (bf16[1024,32]{0,1:T(8,128)(2,1)S(1)}, bf16[1024,32]{0,1:T(8,128)(2,1)}, u32[]{:S(2)}) copy-start(bf16[1024,32]{0,1:T(8,128)(2,1)} %param.32) | copy-start | bytes 196612
  36.8 10.1 %copy-start.2 = (bf16[512,1024]{1,0:T(8,128)(2,1)S(1)}, bf16[512,1024]{1,0:T(8,128)(2,1)}, u32[]{:S(2)}) copy-start(bf16[512,1024]{1,0:T(8,128)(2,1)} %param.18) | copy-start | bytes 3145732
  36.8 97.3 %all-to-all-start = ((bf16[32,32,3072]{2,1,0:T(8,128)(2,1)}), bf16[32,32,3072]{2,1,0:T(8,128)(2,1)}, u32[]{:S(2)}, u32[]{:S(2)}) async-start(bf16[32,32,3072]{2,1,0:T(8,128)(2,1)} %stack.2), calls=%async_computation | async-start | bytes 12582912 | tf_op jit(solution)/shard_map/all_to_all | solution.py:150
  46.9 0.7 copy-start.12
  46.9 0.7 copy-start.13
  208.4 5.0 copy-start.3
  208.4 46.7 %all-to-all-start.2 = ((bf16[4,512,1024]{2,1,0:T(8,128)(2,1)}), bf16[4,512,1024]{2,1,0:T(8,128)(2,1)}, u32[]{:S(2)}, u32[]{:S(2)}) async-start(bf16[4,512,1024]{2,1,0:T(8,128)(2,1)} %broadcast_in_dim.45), calls=%async_computation.2 | async-start | bytes 8388608 | tf_op jit(solution)/shard_map/all_to_all | solution.py:46
  213.4 2.1 copy-start.14
  213.4 2.8 copy-start.15
  255.1 16.2 %all-to-all-start.4 = ((bf16[4,128,1024]{2,1,0:T(8,128)(2,1)}), bf16[4,128,1024]{2,1,0:T(8,128)(2,1)}, u32[]{:S(2)}, u32[]{:S(2)}) async-start(bf16[4,128,1024]{2,1,0:T(8,128)(2,1)} %bitcast.237), calls=%async_computation.4 | async-start | bytes 2097152 | tf_op jit(solution)/shard_map/all_to_all | solution.py:175
  271.3 24.3 %all-to-all-start.3 = ((bf16[4,64,1024]{2,1,0:T(8,128)(2,1)}), bf16[4,64,1024]{2,1,0:T(8,128)(2,1)S(1)}, u32[]{:S(2)}, u32[]{:S(2)}) async-start(bf16[4,64,1024]{2,1,0:T(8,128)(2,1)} %bitcast.21), calls=%async_computation.3 | async-start | bytes 1048576 | tf_op jit(solution)/shard_map/all_to_all | solution.py:208
  300.1 48.9 %all-to-all-start.5 = ((bf16[4,512,1024]{1,2,0:T(8,128)(2,1)}), bf16[4,512,1024]{1,2,0:T(8,128)(2,1)}, u32[]{:S(2)}, u32[]{:S(2)}) async-start(bf16[4,512,1024]{1,2,0:T(8,128)(2,1)} %broadcast_in_dim.46), calls=%async_computation.5 | async-start | bytes 8388608 | tf_op jit(solution)/shard_map/all_to_all | solution.py:46
  305.6 1.2 copy-start.11
  383.6 24.2 %all-to-all-start.6 = ((bf16[4,512,512]{1,2,0:T(8,128)(2,1)}), bf16[4,512,512]{1,2,0:T(8,128)(2,1)}, u32[]{:S(2)}, u32[]{:S(2)}) async-start(bf16[4,512,512]{1,2,0:T(8,128)(2,1)} %broadcast_in_dim.49), calls=%async_computation.6 | async-start | bytes 4194304 | tf_op jit(solution)/shard_map/all_to_all | solution.py:46
  415.5 46.2 %slice-start.4 = ((s8[6291456]{0:T(1024)(128)(4,1)}), s8[4194304]{0:T(1024)(128)(4,1)S(1)}, s32[]{:S(2)}) async-start(s8[6291456]{0:T(1024)(128)(4,1)} %bitcast.252), calls=%async_computation.22 | async-start | bytes 8388608
  415.9 45.9 %slice-start.5 = ((s8[6291456]{0:T(1024)(128)(4,1)}), s8[2097152]{0:T(1024)(128)(4,1)S(1)}, s32[]{:S(2)}) async-start(s8[6291456]{0:T(1024)(128)(4,1)} %bitcast.252), calls=%async_computation.23 | async-start | bytes 4194304
  475.6 22.5 %all-to-all-start.9 = ((bf16[4,512,512]{1,2,0:T(8,128)(2,1)}), bf16[4,512,512]{1,2,0:T(8,128)(2,1)}, u32[]{:S(2)}, u32[]{:S(2)}) async-start(bf16[4,512,512]{1,2,0:T(8,128)(2,1)} %broadcast_in_dim.53), calls=%async_computation.9 | async-start | bytes 4194304 | tf_op jit(solution)/shard_map/all_to_all | solution.py:46
  480.1 18.0 %copy-start.4 = (bf16[512,1024]{1,0:T(8,128)(2,1)S(1)}, bf16[512,1024]{1,0:T(8,128)(2,1)}, u32[]{:S(2)}) copy-start(bf16[512,1024]{1,0:T(8,128)(2,1)} %add_convert_fusion.3) | copy-start | bytes 3145732
  503.3 1.0 copy-start.5
  503.8 43.9 %slice-start.2 = ((s8[6291456]{0:T(1024)(128)(4,1)}), s8[4194304]{0:T(1024)(128)(4,1)S(1)}, s32[]{:S(2)}) async-start(s8[6291456]{0:T(1024)(128)(4,1)} %bitcast.249), calls=%async_computation.20 | async-start | bytes 8388608
  504.3 43.5 %slice-start.3 = ((s8[6291456]{0:T(1024)(128)(4,1)}), s8[2097152]{0:T(1024)(128)(4,1)S(1)}, s32[]{:S(2)}) async-start(s8[6291456]{0:T(1024)(128)(4,1)} %bitcast.249), calls=%async_computation.21 | async-start | bytes 4194304
  561.7 20.4 %all-to-all-start.11 = ((bf16[4,512,512]{1,2,0:T(8,128)(2,1)}), bf16[4,512,512]{1,2,0:T(8,128)(2,1)}, u32[]{:S(2)}, u32[]{:S(2)}) async-start(bf16[4,512,512]{1,2,0:T(8,128)(2,1)} %broadcast_in_dim.55), calls=%async_computation.11 | async-start | bytes 4194304 | tf_op jit(solution)/shard_map/all_to_all | solution.py:46
  566.1 15.9 %copy-start.6 = (bf16[512,1024]{1,0:T(8,128)(2,1)S(1)}, bf16[512,1024]{1,0:T(8,128)(2,1)}, u32[]{:S(2)}) copy-start(bf16[512,1024]{1,0:T(8,128)(2,1)} %copy-done.5) | copy-start | bytes 3145732
  587.8 41.7 %slice-start = ((s8[6291456]{0:T(1024)(128)(4,1)}), s8[4194304]{0:T(1024)(128)(4,1)S(1)}, s32[]{:S(2)}) async-start(s8[6291456]{0:T(1024)(128)(4,1)} %bitcast.246), calls=%async_computation.18 | async-start | bytes 8388608
  588.2 41.4 %slice-start.1 = ((s8[6291456]{0:T(1024)(128)(4,1)}), s8[2097152]{0:T(1024)(128)(4,1)S(1)}, s32[]{:S(2)}) async-start(s8[6291456]{0:T(1024)(128)(4,1)} %bitcast.246), calls=%async_computation.19 | async-start | bytes 4194304
  643.5 18.9 %all-to-all-start.13 = ((bf16[4,512,512]{1,2,0:T(8,128)(2,1)}), bf16[4,512,512]{1,2,0:T(8,128)(2,1)S(1)}, u32[]{:S(2)}, u32[]{:S(2)}) async-start(bf16[4,512,512]{1,2,0:T(8,128)(2,1)} %broadcast_in_dim.57), calls=%async_computation.13 | async-start | bytes 4194304 | tf_op jit(solution)/shard_map/all_to_all | solution.py:46
  668.0 3.7 copy-start.16
  668.0 122.4 %all-to-all-start.14 = ((bf16[4,128,1024]{2,1,0:T(8,128)(2,1)}), bf16[4,128,1024]{2,1,0:T(8,128)(2,1)S(1)}, u32[]{:S(2)}, u32[]{:S(2)}) async-start(bf16[4,128,1024]{2,1,0:T(8,128)(2,1)} %bitcast.274), calls=%async_computation.14 | async-start | bytes 2097152 | tf_op jit(solution)/shard_map/all_to_all | solution.py:243
  790.3 2.4 copy-start.1
Sparse Core Ops, SparseCore 0:
  10.2 116.0 all-gather.4
  128.6 98.6 all-gather.6
  229.6 77.5 all-gather.8
